TPU v7x, 256 devices: a 4x2x16 block of a 4x16x16 slice. The times are simulated.
256 devices in a mesh: groups: 2 (over y), context: 128 (over x, z, core).
Axes of the slice: x: 4, y: 2, z: 16, core: 2. Of those that a mesh axis runs over, the one named last changes fastest.
The devices are a block of a 4x16x16 slice.
Arguments:
- query_proj: bfloat16 [32768, 5120], P(('groups', 'context')), parts along dimension 0, may hold values from -100 to 100
- key_proj: bfloat16 [32768, 1024], P(('groups', 'context')), parts along dimension 0, may hold values from -100 to 100
- values: bfloat16 [32768, 1024], P(('groups', 'context')), parts along dimension 0, may hold values from -6 to 6
- grad_out: bfloat16 [32768, 5120], P(('groups', 'context')), parts along dimension 0, may hold values from -6 to 6
- query_gain: float32 [5120], replicated, may hold values from 0.1 to 1.9
- key_gain: float32 [1024], replicated, may hold values from 0.1 to 1.9
- segments: int32 [32768], P('groups'), parts along dimension 0, may hold values from 0 to 63, never falling along the last dimension, each value on 1 to 512 neighbouring positions
- layout: int32 [512], P('groups'), parts along dimension 0, may hold values from 0 to 255, as said below
Outputs:
- query_grad: bfloat16 [32768, 5120], P(('groups', 'context')), parts along dimension 0
- key_grad: bfloat16 [32768, 1024], P(('groups', 'context')), parts along dimension 0
- value_grad: bfloat16 [32768, 1024], P(('groups', 'context')), parts along dimension 0
- query_gain_grad: float32 [10240], P('groups'), parts along dimension 0
- key_gain_grad: float32 [2048], P('groups'), parts along dimension 0
There are 2 independent parts, one for each index of `groups`. A program takes and returns all parts, laid end to end along the dimension named above; an argument that names none is the same for every part. Nothing has to cross between parts.
Inputs may be any that keep to these rules, and one draw needn't show every extreme that they name: layout is a permutation of the spans; slots are ordered device by device, 2 to a device, and each aligned run of 8 slots holds the spans of one sequence of 512 positions in some order. `segments`: document numbers never fall along the stream; a document has 1 to 512 positions, and one has exactly 512.
All inputs are finite; a program needn't handle non-finite values.
Results may differ from a plain program's by a relative error of at most 0.0086.
Values may be sent and summed in bfloat16 or wider, within the bound.
A program may use at most 128 MiB of HBM per device.

v0:
```python
import jax
import jax.numpy as jnp
from jax import lax
from jax.sharding import Mesh
from jax.sharding import PartitionSpec as P

QUERY_HEADS = 40
KEY_VALUE_HEADS = 8
HEAD_SIZE = 128
SPAN = 64
SEQ_BITS = 2
SEQ_DEVS = 4
LENGTH = 512
CONTEXT = ("context_0", "context_1", "context_2")
GROUPS_CONTEXT = ("groups", "context_0", "context_1", "context_2")
NORM_EPS = 1e-06
ROPE_BASE = 500000.0


def swapped(block, axis, apart):
    count = lax.axis_size(axis)
    route = []
    for low in range(count):
        high = low | 1 << apart
        if high != low and high < count:
            route += [(low, high), (high, low)]
    return lax.ppermute(block, axis, route)


def for_sending(array):

    def short(part):
        return part.astype(jnp.bfloat16) if part.dtype == jnp.float32 else part

    return jax.tree.map(short, array)


def by_axis(array, axes):
    for axis in axes:
        array = lax.psum(array, axis)
    return array


def rope_angles(positions, head_dim):
    half_dim = head_dim // 2
    inv_freq = jnp.power(ROPE_BASE, -2.0 * jnp.arange(half_dim, dtype=jnp.float32) / head_dim)
    angles = positions.astype(jnp.float32)[:, None] * inv_freq[None, :]
    return (jnp.cos(angles), jnp.sin(angles))


def rotate(inputs, cosine, sine, sign_flip):
    tok_rows = inputs.shape[0]
    half_dim = cosine.shape[1]
    halves = inputs.reshape(tok_rows, inputs.shape[1] // (2 * half_dim), 2, half_dim)
    lower_half = halves[:, :, 0]
    upper_half = halves[:, :, 1]
    cosine_b = cosine[:, None, :]
    sine_b = sine[:, None, :] * sign_flip
    rotated = jnp.stack(
        [lower_half * cosine_b - upper_half * sine_b, upper_half * cosine_b + lower_half * sine_b],
        axis=2,
    )
    return rotated.reshape(tok_rows, inputs.shape[1])


def norm_forward(inputs, gain_row):
    mean_sq = jnp.mean(inputs * inputs, axis=1, keepdims=True)
    factor = lax.rsqrt(mean_sq + NORM_EPS)
    return (inputs * factor * gain_row[None, :], factor)


def norm_backward(inputs, factor, gain_row, upstream):
    weighted = upstream * gain_row[None, :]
    inner_sum = jnp.mean(weighted * inputs, axis=1, keepdims=True)
    grad_in = factor * weighted - inputs * factor * factor * factor * inner_sum
    return (grad_in, jnp.sum(upstream * inputs * factor, axis=0))


def head_gradients(queries, key_rows, value_rows, grad_rows, allowed, query_head_group, head_dim):
    tok_rows = queries.shape[0]
    factor = head_dim ** (-0.5)
    query_heads = queries.reshape(tok_rows, query_head_group, head_dim)
    grad_heads = grad_rows.reshape(tok_rows, query_head_group, head_dim)
    scores = (
        jnp.einsum("qgd,kd->gqk", query_heads, key_rows, preferred_element_type=jnp.float32)
        * factor
    )
    scores = jnp.where(allowed[None], scores, -jnp.inf)
    row_max = jnp.max(scores, axis=2, keepdims=True)
    expo = jnp.exp(scores - row_max)
    attn_probs = expo / jnp.sum(expo, axis=2, keepdims=True)
    dprobs = jnp.einsum("qgd,kd->gqk", grad_heads, value_rows, preferred_element_type=jnp.float32)
    row_delta = jnp.sum(attn_probs * dprobs, axis=2, keepdims=True)
    dscores = (attn_probs * (dprobs - row_delta)).astype(jnp.bfloat16)
    probs_low = attn_probs.astype(jnp.bfloat16)
    query_part = (
        jnp.einsum("gqk,kd->qgd", dscores, key_rows, preferred_element_type=jnp.float32) * factor
    )
    key_part = (
        jnp.einsum("gqk,qgd->kd", dscores, query_heads, preferred_element_type=jnp.float32) * factor
    )
    value_part = jnp.einsum(
        "gqk,qgd->kd", probs_low, grad_heads, preferred_element_type=jnp.float32
    )
    return (query_part.reshape(tok_rows, query_head_group * head_dim), key_part, value_part)


def token_info(devices, tok_rows, layout, segments):
    local_index = jnp.arange(tok_rows, dtype=jnp.int32)
    slot_ids = devices[:, None] * (tok_rows // SPAN) + local_index[None, :] // SPAN
    positions = jnp.take(layout, slot_ids) * SPAN + local_index[None, :] % SPAN
    positions = positions.reshape(-1)
    return (positions, jnp.take(segments, positions))


def body(query_proj, key_proj, values, grad_out, query_gain, key_gain, segments, layout):
    tok_rows = query_proj.shape[0]
    my_index = lax.axis_index(CONTEXT)
    query_head_group = QUERY_HEADS // KEY_VALUE_HEADS
    group_width = query_head_group * HEAD_SIZE
    local_rank = my_index % SEQ_DEVS
    seq_base = my_index - local_rank
    positions, doc_query = token_info(jnp.reshape(my_index, (1,)), tok_rows, layout, segments)
    cosine, sine = rope_angles(positions % LENGTH, HEAD_SIZE)
    q_inputs = query_proj.astype(jnp.float32)
    k_inputs = key_proj.astype(jnp.float32)
    q_normed, q_factor = norm_forward(q_inputs, query_gain)
    k_normed, k_factor = norm_forward(k_inputs, key_gain)
    q_rope = rotate(q_normed, cosine, sine, 1.0).astype(jnp.bfloat16)
    k_rope = rotate(k_normed, cosine, sine, 1.0).astype(jnp.bfloat16)
    bit_order = list(range(SEQ_BITS))
    held_k, held_v = (k_rope, values)
    owners = jnp.reshape(local_rank, (1,))
    for bit in bit_order:
        got_k, got_v = swapped((held_k, held_v), CONTEXT, bit)
        held_k = jnp.concatenate([held_k, got_k], axis=0)
        held_v = jnp.concatenate([held_v, got_v], axis=0)
        owners = jnp.concatenate([owners, jnp.bitwise_xor(owners, 1 << bit)])
    pos_key, doc_key = token_info(seq_base + owners, tok_rows, layout, segments)
    allowed = (doc_key[None, :] == doc_query[:, None]) & (pos_key[None, :] <= positions[:, None])
    query_parts, key_parts, value_parts = ([], [], [])
    for key_value_head in range(KEY_VALUE_HEADS):
        query_part, key_part, value_part = head_gradients(
            q_rope[:, key_value_head * group_width : (key_value_head + 1) * group_width],
            held_k[:, key_value_head * HEAD_SIZE : (key_value_head + 1) * HEAD_SIZE],
            held_v[:, key_value_head * HEAD_SIZE : (key_value_head + 1) * HEAD_SIZE],
            grad_out[:, key_value_head * group_width : (key_value_head + 1) * group_width],
            allowed,
            query_head_group,
            HEAD_SIZE,
        )
        query_parts.append(query_part)
        key_parts.append(key_part)
        value_parts.append(value_part)
    dq_rope = jnp.concatenate(query_parts, axis=1)
    dk_all = jnp.concatenate(key_parts, axis=1)
    dv_all = jnp.concatenate(value_parts, axis=1)
    dq_normed = rotate(dq_rope, cosine, sine, -1.0)
    query_grad, q_gain_part = norm_backward(q_inputs, q_factor, query_gain, dq_normed)
    for bit in reversed(bit_order):
        half_rows = dk_all.shape[0] // 2
        back_k, back_v = swapped(
            (for_sending(dk_all[half_rows:]), for_sending(dv_all[half_rows:])), CONTEXT, bit
        )
        dk_all = dk_all[:half_rows] + back_k
        dv_all = dv_all[:half_rows] + back_v
    dk_normed = rotate(dk_all, cosine, sine, -1.0)
    key_grad, k_gain_part = norm_backward(k_inputs, k_factor, key_gain, dk_normed)
    q_gain_total, k_gain_total = (by_axis(q_gain_part, CONTEXT), by_axis(k_gain_part, CONTEXT))
    return (
        query_grad.astype(jnp.bfloat16),
        key_grad.astype(jnp.bfloat16),
        dv_all.astype(jnp.bfloat16),
        q_gain_total,
        k_gain_total,
    )


def solution(mesh):
    split = Mesh(
        mesh.devices.reshape(mesh.shape["groups"], 4, 16, 2),
        ("groups", "context_0", "context_1", "context_2"),
    )
    placed = (
        P(GROUPS_CONTEXT, None),
        P(GROUPS_CONTEXT, None),
        P(GROUPS_CONTEXT, None),
        P(GROUPS_CONTEXT, None),
        P(),
        P(),
        P("groups"),
        P("groups"),
    )
    return jax.shard_map(
        body,
        mesh=split,
        in_specs=placed,
        out_specs=(
            P(GROUPS_CONTEXT, None),
            P(GROUPS_CONTEXT, None),
            P(GROUPS_CONTEXT, None),
            P("groups"),
            P("groups"),
        ),
        check_vma=False,
    )
```

profile of v0, /device:TPU:33, one launch (start us, length us, event | category | flops | bytes accessed | tf_op | source)
XLA Modules:
  0.0 238.2 jit_solution(13967253927241340696)
XLA Ops:
  1.4 3.5 %gather_fusion.1 = s32[512]{0:T(512)S(1)} fusion(s32[256]{0:T(256)S(1)} %copy-done.2, s32[1024]{0:T(1024)S(1)} %pad_clamp_fusion.2), kind=kCustom, calls=%fused_computation.1 | custom fusion | bytes 6144 | tf_op jit(solution)/shard_map/jit(_take)/gather | solution.py:111
  4.9 1.3 gather_fusion
  6.3 1.1 gather_fusion.3
  9.1 20.5 %collective-permute-start = (bf16[128,1024]{1,0:T(8,128)(2,1)S(1)}, bf16[128,1024]{1,0:T(8,128)(2,1)}, u32[]{:S(2)}, u32[]{:S(2)}) collective-permute-start(bf16[128,1024]{1,0:T(8,128)(2,1)S(1)} %copy.74), channel_id=1, source_target_pairs={{0,1},{1,0},{2,3},{3,2},{4,5},{5,4},{6,7},{7,6},{8,9},{9,8},{10,11... | collective-permute-start | bytes 786440 | tf_op jit(solution)/shard_map/ppermute | solution.py:27
  30.0 3.1 %gather_fusion.2 = s32[512]{0:T(512)S(1)} fusion(s32[16384]{0:T(1024)S(1)} %copy-done, s32[1024]{0:T(1024)S(1)} %get-tuple-element.89), kind=kCustom, calls=%fused_computation.2 | custom fusion | bytes 6144 | tf_op jit(solution)/shard_map/jit(_take)/gather | solution.py:113
  34.8 2.2 fusion.9
  38.3 1.2 copy-done.13
  39.5 1.1 fusion.131
  40.5 1.8 pad_maximum_fusion.3
  43.0 1.7 copy.190
  44.7 1.7 copy.191
  46.4 1.1 fusion.130
  47.5 1.9 pad_maximum_fusion.4
  49.4 1.5 collective-permute-start.3
  50.9 1.7 copy.192
  56.7 1.7 constant_dynamic-update-slice_fusion.1
  58.4 1.2 pad_maximum_fusion.2
  59.6 1.6 fusion.132
  61.2 6.0 %collective-permute-done.3 = bf16[256,1024]{1,0:T(8,128)(2,1)} collective-permute-done((bf16[256,1024]{1,0:T(8,128)(2,1)}, bf16[256,1024]{1,0:T(8,128)(2,1)}, u32[]{:S(2)}, u32[]{:S(2)}) %collective-permute-start.3) | collective-permute-done | bytes 524320 | tf_op jit(solution)/shard_map/ppermute | solution.py:27
  67.2 1.9 constant_dynamic-update-slice_fusion
  69.0 1.8 multiply_reduce_fusion.7
  72.4 2.5 %fusion.57 = f32[512,1024]{0,1:T(8,128)} fusion(bf16[128,5,128]{0,2,1:T(8,128)(2,1)} %bitcast.579, f32[5,128]{1,0:T(8,128)S(1)} %get-tuple-element.56, bf16[128,5,128]{0,2,1:T(8,128)(2,1)S(1)} %bitcast.564, pred[128,512]{0,1:T(8,128)(4,1)S(1)} %copy-done.54, bf16[512,1024]{1,0:T(8,128)(2,1)S(1)} %pad_maximum_fusion.2), kind=kOutput, calls=%fused_computation.120 | convolution fusion | flops 169411712 | bytes 790528 | tf_op jit(solution)/shard_map/gqk,qgd->kd/dot_general | solution.py:102
  74.9 1.6 fusion.133
  76.5 1.8 multiply_reduce_fusion.6
  79.2 1.0 fusion.71
  80.3 2.5 %fusion.134 = (f32[5,128]{1,0:T(8,128)S(1)}, f32[5,128,512]{1,2,0:T(8,128)}) fusion(bf16[128,5,128]{0,2,1:T(8,128)(2,1)} %bitcast.556, pred[128,512]{0,1:T(8,128)(4,1)S(1)} %copy-done.54, bf16[512,1024]{1,0:T(8,128)(2,1)S(1)} %pad_maximum_fusion.2), kind=kOutput, calls=%fused_computation.312 | convolution fusion | flops 85197312 | bytes 1673728 | tf_op jit(solution)/shard_map/sub | solution.py:90
  82.8 1.9 multiply_reduce_fusion.5
  86.9 2.5 %fusion.135 = (f32[5,128]{1,0:T(8,128)S(1)}, f32[5,128,512]{1,2,0:T(8,128)}) fusion(bf16[128,5,128]{0,2,1:T(8,128)(2,1)} %bitcast.553, pred[128,512]{0,1:T(8,128)(4,1)S(1)} %copy-done.54, bf16[512,1024]{1,0:T(8,128)(2,1)S(1)} %pad_maximum_fusion.2), kind=kOutput, calls=%fused_computation.313 | convolution fusion | flops 85197312 | bytes 1673728 | tf_op jit(solution)/shard_map/sub | solution.py:90
  89.4 1.9 multiply_reduce_fusion.4
  92.6 1.1 fusion.67
  93.6 2.5 %fusion.136 = (f32[5,128]{1,0:T(8,128)S(1)}, f32[5,128,512]{1,2,0:T(8,128)}) fusion(bf16[128,5,128]{0,2,1:T(8,128)(2,1)} %bitcast.550, pred[128,512]{0,1:T(8,128)(4,1)S(1)} %copy-done.54, bf16[512,1024]{1,0:T(8,128)(2,1)S(1)} %pad_maximum_fusion.2), kind=kOutput, calls=%fused_computation.314 | convolution fusion | flops 85197312 | bytes 1673728 | tf_op jit(solution)/shard_map/sub | solution.py:90
  96.1 1.9 multiply_reduce_fusion.3
  99.3 1.1 fusion.65
  100.3 2.5 %fusion.137 = (f32[5,128]{1,0:T(8,128)S(1)}, f32[5,128,512]{1,2,0:T(8,128)}) fusion(bf16[128,5,128]{0,2,1:T(8,128)(2,1)} %bitcast.547, pred[128,512]{0,1:T(8,128)(4,1)S(1)} %copy-done.54, bf16[512,1024]{1,0:T(8,128)(2,1)S(1)} %pad_maximum_fusion.2), kind=kOutput, calls=%fused_computation.315 | convolution fusion | flops 85197312 | bytes 1673728 | tf_op jit(solution)/shard_map/sub | solution.py:90
  102.8 1.9 multiply_reduce_fusion.2
  104.9 1.1 convolution_multiply_fusion.10
  106.0 1.1 fusion.63
  107.1 2.5 %fusion.138 = (f32[5,128]{1,0:T(8,128)S(1)}, f32[5,128,512]{1,2,0:T(8,128)}) fusion(bf16[128,5,128]{0,2,1:T(8,128)(2,1)} %bitcast.544, pred[128,512]{0,1:T(8,128)(4,1)S(1)} %copy-done.54, bf16[512,1024]{1,0:T(8,128)(2,1)S(1)} %pad_maximum_fusion.2), kind=kOutput, calls=%fused_computation.316 | convolution fusion | flops 85197312 | bytes 1673728 | tf_op jit(solution)/shard_map/sub | solution.py:90
  109.6 1.9 multiply_reduce_fusion.1
  111.7 1.1 convolution_multiply_fusion.9
  113.8 2.5 %fusion.139 = (f32[5,128]{1,0:T(8,128)S(1)}, f32[5,128,512]{1,2,0:T(8,128)}) fusion(bf16[128,5,128]{0,2,1:T(8,128)(2,1)} %bitcast.541, pred[128,512]{0,1:T(8,128)(4,1)S(1)} %copy-done.54, bf16[512,1024]{1,0:T(8,128)(2,1)S(1)} %pad_maximum_fusion.2), kind=kOutput, calls=%fused_computation.317 | convolution fusion | flops 85197312 | bytes 1673728 | tf_op jit(solution)/shard_map/sub | solution.py:90
  116.3 1.9 multiply_reduce_fusion
  119.1 1.1 fusion.59
  120.2 2.1 slice.375
  125.3 1.6 copy-done.3
  126.9 3.0 %fusion.17 = (f32[5120]{0:T(1024)S(1)}, f32[128]{0:T(128)S(1)}) fusion(bf16[128,5120]{0,1:T(8,128)(2,1)S(1)} %copy.70, f32[128,40,2,64]{0,3,2,1:T(8,128)S(1)} %pad_maximum_fusion, f32[128]{0:T(128)S(1)} %add_rsqrt_fusion.1, f32[5120]{0:T(1024)S(1)} %copy-done.44), kind=kLoop, calls=%fused_computation.25 | loop fusion | flops 4582272 | bytes 3974144 | tf_op jit(solution)/shard_map/reduce_sum | solution.py:76
  129.9 1.5 fusion.56
  131.4 1.5 fusion.55
  132.9 1.5 fusion.54
  134.5 1.5 fusion.53
  136.0 1.5 fusion.52
  137.5 1.5 fusion.51
  139.0 1.5 fusion.50
  140.5 2.1 slice.374
  142.6 1.2 collective-permute-start.6
  143.8 3.5 %fusion.13 = bf16[128,5120]{0,1:T(8,128)(2,1)S(1)} fusion(bf16[128,5120]{0,1:T(8,128)(2,1)S(1)} %copy.70, f32[128,40,2,64]{0,3,2,1:T(8,128)} %copy-done.3, f32[128]{0:T(128)S(1)} %broadcast_multiply_fusion.2, f32[5120]{0:T(1024)S(1)} %copy-done.44, f32[128]{0:T(128)S(1)} %add_rsqrt_fusion.1), kind=kLoop, calls=%fused_computation.21 | loop fusion | flops 5898240 | bytes 5264384 | tf_op jit(solution)/shard_map/convert_element_type | solution.py:171
  147.3 1.4 copy.131
  148.8 1.6 slice_add_fusion.1
  150.4 1.7 collective-permute-start.5
  152.1 3.1 %collective-permute-done.6 = bf16[256,1024]{0,1:T(8,128)(2,1)S(1)} collective-permute-done((bf16[256,1024]{0,1:T(8,128)(2,1)}, bf16[256,1024]{0,1:T(8,128)(2,1)S(1)}, u32[]{:S(2)}, u32[]{:S(2)}) %collective-permute-start.6) | collective-permute-done | bytes 524320 | tf_op jit(solution)/shard_map/ppermute | solution.py:27
  155.5 2.0 collective-permute-start.7
  160.6 11.0 %all-reduce.1 = (f32[5120]{0:T(1024)S(1)}, f32[1024]{0:T(1024)S(1)}) all-reduce(f32[5120]{0:T(1024)S(1)} %get-tuple-element.15, f32[1024]{0:T(1024)S(1)} %get-tuple-element.17), channel_id=1, replica_groups=mesh['groups'=2,'context_0'=4,'context_1'=16,'context_2'=2] {'context_0'}, use_global_device_ids=true, to_apply=%region_29.30 | all-reduce | flops 6144 | bytes 49152 | tf_op jit(solution)/shard_map/psum | solution.py:40
  171.6 45.1 %all-reduce = (f32[5120]{0:T(1024)S(1)}, f32[1024]{0:T(1024)S(1)}) all-reduce(f32[5120]{0:T(1024)S(1)} %get-tuple-element.21, f32[1024]{0:T(1024)S(1)} %get-tuple-element.22), channel_id=1, replica_groups=mesh['groups'=2,'context_0'=4,'context_1'=16,'context_2'=2] {'context_1'}, use_global_device_ids=true, to_apply=%region_30.31 | all-reduce | flops 6144 | bytes 49152 | tf_op jit(solution)/shard_map/psum | solution.py:40
  216.7 21.5 %all-reduce.2 = (f32[5120]{0:T(1024)}, f32[1024]{0:T(1024)}) all-reduce(f32[5120]{0:T(1024)S(1)} %get-tuple-element.19, f32[1024]{0:T(1024)S(1)} %get-tuple-element.20), channel_id=1, replica_groups=mesh['groups'=2,'context_0'=4,'context_1'=16,'context_2'=2] {'context_2'}, use_global_device_ids=true, to_apply=%region_31.32 | all-reduce | flops 6144 | bytes 49152 | tf_op jit(solution)/shard_map/psum | solution.py:40
  (197 shorter events, 26.2 us)
Async XLA Ops:
  0.6 5.7 %copy-start = (s32[16384]{0:T(1024)S(1)}, s32[16384]{0:T(1024)}, u32[]{:S(2)}) copy-start(s32[16384]{0:T(1024)} %param.14) | copy-start | bytes 196612
  0.6 0.7 copy-start.2
  1.4 6.1 %copy-start.43 = (bf16[128,1024]{1,0:T(8,128)(2,1)S(1)}, bf16[128,1024]{1,0:T(8,128)(2,1)}, u32[]{:S(2)}) copy-start(bf16[128,1024]{1,0:T(8,128)(2,1)} %param.9) | copy-start | bytes 786436
  4.9 3.8 %copy-start.55 = (f32[1024]{0:T(1024)S(1)}, f32[1024]{0:T(1024)}, u32[]{:S(2)}) copy-start(f32[1024]{0:T(1024)} %param.13) | copy-start | bytes 12292
  8.6 21.0 %copy-start.20 = (bf16[128,1024]{1,0:T(8,128)(2,1)S(1)}, bf16[128,1024]{1,0:T(8,128)(2,1)}, u32[]{:S(2)}) copy-start(bf16[128,1024]{1,0:T(8,128)(2,1)} %param.10) | copy-start | bytes 786436
  9.0 24.3 %copy-start.12 = (bf16[128,5120]{1,0:T(8,128)(2,1)S(1)}, bf16[128,5120]{1,0:T(8,128)(2,1)}, u32[]{:S(2)}) copy-start(bf16[128,5120]{1,0:T(8,128)(2,1)} %param.8) | copy-start | bytes 3932164
  9.1 31.4 %collective-permute-start = (bf16[128,1024]{1,0:T(8,128)(2,1)S(1)}, bf16[128,1024]{1,0:T(8,128)(2,1)}, u32[]{:S(2)}, u32[]{:S(2)}) collective-permute-start(bf16[128,1024]{1,0:T(8,128)(2,1)S(1)} %copy.74), channel_id=1, source_target_pairs={{0,1},{1,0},{2,3},{3,2},{4,5},{5,4},{6,7},{7,6},{8,9},{9,8},{10,11... | collective-permute-start | bytes 786440 | tf_op jit(solution)/shard_map/ppermute | solution.py:27
  29.7 17.9 %collective-permute-start.2 = (bf16[128,1024]{1,0:T(8,128)(2,1)S(1)}, bf16[128,1024]{1,0:T(8,128)(2,1)}, u32[]{:S(2)}, u32[]{:S(2)}) collective-permute-start(bf16[128,1024]{1,0:T(8,128)(2,1)S(1)} %copy-done.20), channel_id=1, source_target_pairs={{0,1},{1,0},{2,3},{3,2},{4,5},{5,4},{6,7},{7,6},{8,9},{9,8},{10,11... | collective-permute-start | bytes 786440 | tf_op jit(solution)/shard_map/ppermute | solution.py:27
  34.0 0.7 copy-start.44
  38.1 1.3 copy-start.13
  42.3 16.1 %collective-permute-start.1 = (bf16[256,1024]{1,0:T(8,128)(2,1)}, bf16[256,1024]{1,0:T(8,128)(2,1)}, u32[]{:S(2)}, u32[]{:S(2)}) collective-permute-start(bf16[256,1024]{1,0:T(8,128)(2,1)} %pad_maximum_fusion.3), channel_id=1, source_target_pairs={{0,2},{2,0},{1,3},{3,1},{4,6},{6,4},{5,7},{7,5},{8,10},{10,8},{9,1... | collective-permute-start | bytes 1572872 | tf_op jit(solution)/shard_map/ppermute | solution.py:27
  47.5 5.1 %copy-start.25 = (bf16[128,640]{1,0:T(8,128)(2,1)S(1)}, bf16[128,640]{1,0:T(8,128)(2,1)}, u32[]{:S(2)}) copy-start(bf16[128,640]{1,0:T(8,128)(2,1)} %get-tuple-element.45) | copy-start | bytes 491524
  47.5 5.9 %copy-start.24 = (bf16[128,640]{1,0:T(8,128)(2,1)S(1)}, bf16[128,640]{1,0:T(8,128)(2,1)}, u32[]{:S(2)}) copy-start(bf16[128,640]{1,0:T(8,128)(2,1)} %get-tuple-element.44) | copy-start | bytes 491524
  47.5 6.7 %copy-start.23 = (bf16[128,640]{1,0:T(8,128)(2,1)S(1)}, bf16[128,640]{1,0:T(8,128)(2,1)}, u32[]{:S(2)}) copy-start(bf16[128,640]{1,0:T(8,128)(2,1)} %get-tuple-element.43) | copy-start | bytes 491524
  47.5 7.5 %copy-start.22 = (bf16[128,640]{1,0:T(8,128)(2,1)S(1)}, bf16[128,640]{1,0:T(8,128)(2,1)}, u32[]{:S(2)}) copy-start(bf16[128,640]{1,0:T(8,128)(2,1)} %get-tuple-element.42) | copy-start | bytes 491524
  47.5 8.3 %copy-start.21 = (bf16[128,640]{1,0:T(8,128)(2,1)S(1)}, bf16[128,640]{1,0:T(8,128)(2,1)}, u32[]{:S(2)}) copy-start(bf16[128,640]{1,0:T(8,128)(2,1)} %get-tuple-element.41) | copy-start | bytes 491524
  49.4 17.8 %collective-permute-start.3 = (bf16[256,1024]{1,0:T(8,128)(2,1)}, bf16[256,1024]{1,0:T(8,128)(2,1)}, u32[]{:S(2)}, u32[]{:S(2)}) collective-permute-start(bf16[256,1024]{1,0:T(8,128)(2,1)} %pad_maximum_fusion.4), channel_id=1, source_target_pairs={{0,2},{2,0},{1,3},{3,1},{4,6},{6,4},{5,7},{7,5},{8,10},{10,8},{9,1... | collective-permute-start | bytes 1572872 | tf_op jit(solution)/shard_map/ppermute | solution.py:27
  56.7 2.9 %copy-start.41 = (bf16[128,640]{0,1:T(8,128)(2,1)S(1)}, bf16[128,640]{0,1:T(8,128)(2,1)}, u32[]{:S(2)}) copy-start(bf16[128,640]{0,1:T(8,128)(2,1)} %get-tuple-element.40) | copy-start | bytes 491524
  56.7 2.9 %copy-start.54 = (pred[128,512]{0,1:T(8,128)(4,1)S(1)}, pred[128,512]{0,1:T(8,128)(4,1)}, u32[]{:S(2)}) copy-start(pred[128,512]{0,1:T(8,128)(4,1)} %compare_and_fusion) | copy-start | bytes 196612
  59.6 9.5 %copy-start.53 = (bf16[128,640]{0,1:T(8,128)(2,1)S(1)}, bf16[128,640]{0,1:T(8,128)(2,1)}, u32[]{:S(2)}) copy-start(bf16[128,640]{0,1:T(8,128)(2,1)} %copy.190) | copy-start | bytes 491524
  69.0 1.8 copy-start.4
  72.4 2.5 %copy-start.38 = (bf16[128,640]{0,1:T(8,128)(2,1)S(1)}, bf16[128,640]{0,1:T(8,128)(2,1)}, u32[]{:S(2)}) copy-start(bf16[128,640]{0,1:T(8,128)(2,1)} %get-tuple-element.39) | copy-start | bytes 491524
  74.9 1.6 copy-start.46
  76.5 1.8 copy-start.6
  78.3 0.9 copy-start.39
  82.8 1.9 copy-start.7
  84.7 1.2 copy-start.36
  89.4 1.9 copy-start.8
  91.3 1.2 copy-start.34
  96.1 1.9 copy-start.9
  98.0 1.2 copy-start.32
  102.8 1.9 copy-start.10
  104.7 1.3 copy-start.30
  109.6 1.9 copy-start.11
  111.5 1.3 copy-start.28
  116.3 1.9 copy-start.5
  118.2 0.9 copy-start.26
  120.2 2.5 %copy-start.14 = (f32[128,5,128]{2,0,1:T(8,128)S(1)}, f32[128,5,128]{2,0,1:T(8,128)}, u32[]{:S(2)}) copy-start(f32[128,5,128]{2,0,1:T(8,128)} %convolution_multiply_fusion.13) | copy-start | bytes 983044
  120.2 2.6 %copy-start.15 = (f32[128,5,128]{2,0,1:T(8,128)S(1)}, f32[128,5,128]{2,0,1:T(8,128)}, u32[]{:S(2)}) copy-start(f32[128,5,128]{2,0,1:T(8,128)} %convolution_multiply_fusion.12) | copy-start | bytes 983044
  122.3 26.4 %collective-permute-start.4 = (bf16[256,1024]{0,1:T(8,128)(2,1)}, bf16[256,1024]{0,1:T(8,128)(2,1)}, u32[]{:S(2)}, u32[]{:S(2)}) collective-permute-start(bf16[256,1024]{0,1:T(8,128)(2,1)} %slice.375), channel_id=1, source_target_pairs={{0,2},{2,0},{1,3},{3,1},{4,6},{6,4},{5,7},{7,5},{8,10},{10,8},{9,1... | collective-permute-start | bytes 1572872 | tf_op jit(solution)/shard_map/ppermute | solution.py:27
  122.6 1.0 copy-start.16
  122.7 1.1 copy-start.17
  122.7 1.1 copy-start.18
  123.6 0.8 copy-start.42
  125.3 1.6 copy-start.3
  126.9 3.0 %copy-start.40 = (bf16[128,640]{0,1:T(8,128)(2,1)S(1)}, bf16[128,640]{0,1:T(8,128)(2,1)}, u32[]{:S(2)}) copy-start(bf16[128,640]{0,1:T(8,128)(2,1)} %get-tuple-element.39) | copy-start | bytes 491524
  126.9 3.0 %copy-start.47 = (bf16[128,640]{0,1:T(8,128)(2,1)S(1)}, bf16[128,640]{0,1:T(8,128)(2,1)}, u32[]{:S(2)}) copy-start(bf16[128,640]{0,1:T(8,128)(2,1)} %copy.191) | copy-start | bytes 491524
  129.9 1.5 copy-start.37
  129.9 1.5 copy-start.52
  131.4 1.5 copy-start.35
  131.4 1.5 copy-start.51
  132.9 1.5 copy-start.33
  132.9 1.5 copy-start.50
  134.5 1.5 copy-start.31
  134.5 1.5 copy-start.49
  136.0 1.5 copy-start.29
  136.0 1.5 copy-start.48
  137.5 1.5 copy-start.27
  137.5 1.5 copy-start.45
  142.6 12.7 %collective-permute-start.6 = (bf16[256,1024]{0,1:T(8,128)(2,1)}, bf16[256,1024]{0,1:T(8,128)(2,1)S(1)}, u32[]{:S(2)}, u32[]{:S(2)}) collective-permute-start(bf16[256,1024]{0,1:T(8,128)(2,1)} %slice.374), channel_id=1, source_target_pairs={{0,2},{2,0},{1,3},{3,1},{4,6},{6,4},{5,7},{7,5},{8,10},{10,8},{9,1... | collective-permute-start | bytes 1572872 | tf_op jit(solution)/shard_map/ppermute | solution.py:27
  148.8 6.5 %copy-start.19 = (f32[512,1024]{0,1:T(8,128)S(1)}, f32[512,1024]{0,1:T(8,128)}, u32[]{:S(2)}) copy-start(f32[512,1024]{0,1:T(8,128)} %fusion.50) | copy-start | bytes 6291460
  150.4 7.1 %collective-permute-start.5 = (bf16[128,1024]{0,1:T(8,128)(2,1)S(1)}, bf16[128,1024]{0,1:T(8,128)(2,1)S(1)}, u32[]{:S(2)}, u32[]{:S(2)}) collective-permute-start(bf16[128,1024]{0,1:T(8,128)(2,1)S(1)} %slice.377), channel_id=1, source_target_pairs={{0,1},{1,0},{2,3},{3,2},{4,5},{5,4},{6,7},{7,6},{8,9},{9,8},{10,11... | collective-permute-start | bytes 786440 | tf_op jit(solution)/shard_map/ppermute | solution.py:27
  155.5 3.2 %collective-permute-start.7 = (bf16[128,1024]{0,1:T(8,128)(2,1)S(1)}, bf16[128,1024]{0,1:T(8,128)(2,1)S(1)}, u32[]{:S(2)}, u32[]{:S(2)}) collective-permute-start(bf16[128,1024]{0,1:T(8,128)(2,1)S(1)} %slice.376), channel_id=1, source_target_pairs={{0,1},{1,0},{2,3},{3,2},{4,5},{5,4},{6,7},{7,6},{8,9},{9,8},{10,11... | collective-permute-start | bytes 786440 | tf_op jit(solution)/shard_map/ppermute | solution.py:27
  158.7 79.5 %copy-start.1 = (s32[16384]{0:T(1024)S(1)}, s32[16384]{0:T(1024)}, u32[]{:S(2)}) copy-start(s32[16384]{0:T(1024)} %param.14) | copy-start | bytes 196612
where the time goes:
time: 239 us; the launch traced here: 238 us
  blocking collectives  77.5 us (32%)
  matrix products  60.7 us (25%)
  local copies, waits for them, and re-layouts  39.1 us (16%)
  starting transfers between devices  27.5 us (12%)
  other arithmetic  22.1 us (9%)
  waiting for transfers between devices  9.75 us (4%)
    psum x3, blocking collectives, by_axis(): array = lax.psum(array, axis)  77.5 us
    ppermute x8, starting transfers between devices, swapped(): return lax.ppermute(block, axis, route)  27.5 us
    unnamed x134, local copies, waits for them, and re-layouts  21.6 us
    sub x8, matrix products, head_gradients(): expo = jnp.exp(scores - row_max)  18.1 us
    dot_general x8, matrix products, head_gradients(): jnp.einsum('qgd,kd->gqk', grad_heads, value_rows, preferred_element_type=...  15 us
    dot_general x8, matrix products, head_gradients(): jnp.einsum('gqk,qgd->kd', probs_low, grad_heads, preferred_element_type=j...  13 us
    ppermute x8, waiting for transfers between devices, swapped(): return lax.ppermute(block, axis, route)  9.75 us
    dot_general x8, matrix products, head_gradients(): jnp.einsum('gqk,qgd->kd', dscores, query_heads, preferred_element_type=jn...  8.41 us
  transfers between devices with their start and end apart: 8, of which 3 were waited for; matrix products, arithmetic and copies ran while one was open for 22% of the time, Pallas kernels for 0%

commit v1 on v0

--- a/solution.py
+++ b/solution.py
@@ -37,7 +37,7 @@
 
 def by_axis(array, axes):
     for axis in axes:
-        array = lax.psum(array, axis)
+        array = jnp.sum(lax.all_gather(array, axis), axis=0)
     return array
 
 

time: 239 us -> 258 us (1.079)
  blocking collectives: 77.5 us -> 87.3 us
  matrix products: 60.7 us -> 68.4 us
  other arithmetic: 22.1 us -> 26.1 us
  starting transfers between devices: 27.5 us -> 24.6 us
    all_gather x0 -> x6, blocking collectives: none -> 87.3 us  [by_axis(): array = jnp.sum(lax.all_gather(array, axis), axis=0)]
    psum x3 -> x0, blocking collectives: 77.5 us -> none  [by_axis(): array = lax.psum(array, axis)]
    dot_general x8, matrix products: 13 us -> 19.6 us  [head_gradients(): jnp.einsum('gqk,qgd->kd', probs_low, grad_heads, preferred_element_type=j...]
    dot_general x8, matrix products: 6.18 us -> 12.4 us  [head_gradients(): jnp.einsum('gqk,kd->qgd', dscores, key_rows, preferred_element_type=jnp.f...]
    dot_general x8, matrix products: 8.41 us -> 3.47 us  [head_gradients(): jnp.einsum('gqk,qgd->kd', dscores, query_heads, preferred_element_type=jn...]
    ppermute x8, starting transfers between devices: 27.5 us -> 24.6 us  [swapped(): return lax.ppermute(block, axis, route)]
    unnamed x134 -> x190, local copies, waits for them, and re-layouts: 21.6 us -> 24 us
  transfers between devices with their start and end apart: 8 -> 8, of which waited for: 3 -> 2; matrix products, arithmetic and copies ran while one was open for 22% -> 22% of each run, Pallas kernels for 0% -> 0%
where the time goes in v1:
time: 258 us; the launch traced here: 256 us
  blocking collectives  87.3 us (34%)
  matrix products  68.4 us (27%)
  local copies, waits for them, and re-layouts  41 us (16%)
  other arithmetic  26.1 us (10%)
  starting transfers between devices  24.6 us (10%)
  waiting for transfers between devices  7.2 us (3%)
    all_gather x6, blocking collectives, by_axis(): array = jnp.sum(lax.all_gather(array, axis), axis=0)  87.3 us
    ppermute x8, starting transfers between devices, swapped(): return lax.ppermute(block, axis, route)  24.6 us
    unnamed x190, local copies, waits for them, and re-layouts  24 us
    dot_general x8, matrix products, head_gradients(): jnp.einsum('gqk,qgd->kd', probs_low, grad_heads, preferred_element_type=j...  19.6 us
    sub x8, matrix products, head_gradients(): expo = jnp.exp(scores - row_max)  18 us
    dot_general x8, matrix products, head_gradients(): jnp.einsum('qgd,kd->gqk', grad_heads, value_rows, preferred_element_type=...  15 us
    dot_general x8, matrix products, head_gradients(): jnp.einsum('gqk,kd->qgd', dscores, key_rows, preferred_element_type=jnp.f...  12.4 us
    ppermute x8, waiting for transfers between devices, swapped(): return lax.ppermute(block, axis, route)  7.2 us
  transfers between devices with their start and end apart: 8, of which 2 were waited for; matrix products, arithmetic and copies ran while one was open for 22% of the time, Pallas kernels for 0%

profile of v1, /device:TPU:33, one launch (start us, length us, event | category | flops | bytes accessed | tf_op | source)
XLA Modules:
  0.0 256.4 jit_solution(13349108493785950345)
XLA Ops:
  0.8 1.6 gather_fusion
  2.7 3.5 %gather_fusion.1 = s32[512]{0:T(512)S(1)} fusion(s32[256]{0:T(256)S(1)} %copy-done.2, s32[1024]{0:T(1024)S(1)} %pad_clamp_fusion.2), kind=kCustom, calls=%fused_computation.1 | custom fusion | bytes 6144 | tf_op jit(solution)/shard_map/jit(_take)/gather | solution.py:111
  6.4 1.1 gather_fusion.3
  9.7 20.5 %collective-permute-start = (bf16[128,1024]{1,0:T(8,128)(2,1)S(1)}, bf16[128,1024]{1,0:T(8,128)(2,1)}, u32[]{:S(2)}, u32[]{:S(2)}) collective-permute-start(bf16[128,1024]{1,0:T(8,128)(2,1)S(1)} %copy.202), channel_id=1, source_target_pairs={{0,1},{1,0},{2,3},{3,2},{4,5},{5,4},{6,7},{7,6},{8,9},{9,8},{10,11... | collective-permute-start | bytes 786440 | tf_op jit(solution)/shard_map/ppermute | solution.py:27
  32.1 2.2 fusion.9
  34.3 1.4 subtract_convert_fusion
  35.7 3.1 %gather_fusion.2 = s32[512]{0:T(512)S(1)} fusion(s32[16384]{0:T(1024)S(1)} %copy-done, s32[1024]{0:T(1024)S(1)} %get-tuple-element.93), kind=kCustom, calls=%fused_computation.2 | custom fusion | bytes 6144 | tf_op jit(solution)/shard_map/jit(_take)/gather | solution.py:113
  39.2 1.5 pad_maximum_fusion.1
  40.9 1.1 fusion.131
  42.0 1.8 pad_maximum_fusion.3
  44.5 1.7 copy.318
  46.2 1.7 copy.319
  48.0 1.1 fusion.130
  49.1 1.9 pad_maximum_fusion.4
  50.9 1.5 collective-permute-start.3
  57.2 1.7 constant_dynamic-update-slice_fusion.1
  59.0 1.2 pad_maximum_fusion.2
  60.2 1.6 fusion.132
  61.8 6.6 %collective-permute-done.3 = bf16[256,1024]{1,0:T(8,128)(2,1)} collective-permute-done((bf16[256,1024]{1,0:T(8,128)(2,1)}, bf16[256,1024]{1,0:T(8,128)(2,1)}, u32[]{:S(2)}, u32[]{:S(2)}) %collective-permute-start.3) | collective-permute-done | bytes 524320 | tf_op jit(solution)/shard_map/ppermute | solution.py:27
  68.4 1.9 constant_dynamic-update-slice_fusion
  70.3 1.8 multiply_reduce_fusion.7
  72.3 1.0 convolution_multiply_fusion.15
  73.4 1.1 fusion.73
  74.4 2.5 fusion.57
  77.7 1.6 fusion.133
  79.3 1.8 multiply_reduce_fusion.6
  82.3 2.5 fusion.134
  84.8 1.9 multiply_reduce_fusion.5
  86.9 1.2 convolution_multiply_fusion.13
  88.2 2.5 fusion.135
  90.6 1.9 multiply_reduce_fusion.4
  93.6 1.9 convolution_multiply_fusion.12
  95.6 2.5 fusion.136
  98.1 1.9 multiply_reduce_fusion.3
  101.0 1.9 convolution_multiply_fusion.11
  102.9 2.5 fusion.137
  105.4 1.9 multiply_reduce_fusion.2
  108.4 1.9 convolution_multiply_fusion.10
  110.3 2.5 fusion.138
  112.8 1.9 multiply_reduce_fusion.1
  115.8 2.0 convolution_multiply_fusion.9
  117.7 2.5 fusion.139
  120.2 1.9 multiply_reduce_fusion
  122.4 1.4 convolution_multiply_fusion.8
  126.5 3.2 %fusion.17 = (f32[5120]{0:T(1024)S(1)}, f32[128]{0:T(128)S(1)}) fusion(bf16[128,5120]{0,1:T(8,128)(2,1)S(1)} %copy.198, f32[128,40,2,64]{0,3,2,1:T(8,128)S(1)} %pad_maximum_fusion, f32[128]{0:T(128)S(1)} %copy-done.76, f32[5120]{0:T(1024)S(1)} %copy-done.61), kind=kLoop, calls=%fused_computation.25 | loop fusion | flops 4582272 | bytes 3974144 | tf_op jit(solution)/shard_map/reduce_sum | solution.py:76
  133.2 1.4 copy-done.17
  135.8 2.4 fusion.56
  138.2 2.5 fusion.55
  140.7 2.4 fusion.54
  143.1 2.4 fusion.53
  145.6 2.5 fusion.52
  148.0 2.4 fusion.51
  150.5 2.4 fusion.50
  152.9 2.1 slice.374
  155.0 1.2 collective-permute-start.6
  156.1 3.5 %fusion.13 = bf16[128,5120]{0,1:T(8,128)(2,1)S(1)} fusion(bf16[128,5120]{0,1:T(8,128)(2,1)S(1)} %copy.198, f32[128,40,2,64]{0,3,2,1:T(8,128)} %copy-done.3, f32[128]{0:T(128)S(1)} %broadcast_multiply_fusion.2, f32[5120]{0:T(1024)S(1)} %copy-done.61, f32[128]{0:T(128)S(1)} %copy-done.76), kind=kLoop, calls=%fused_computation.21 | loop fusion | flops 5898240 | bytes 5264384 | tf_op jit(solution)/shard_map/convert_element_type | solution.py:171
  159.6 1.4 copy.259
  161.1 9.0 %all-gather = f32[20480]{0:T(1024)S(1)} all-gather(f32[5120]{0:T(1024)S(1)} %get-tuple-element.25), channel_id=2, replica_groups=mesh['groups'=2,'context_0'=4,'context_1'=16,'context_2'=2] {'context_0'}, dimensions={0}, use_global_device_ids=true | all-gather | bytes 102400 | tf_op jit(solution)/shard_map/all_gather | solution.py:40
  170.2 25.0 %all-gather.1 = f32[81920]{0:T(1024)S(1)} all-gather(f32[5120]{0:T(1024)S(1)} %reduce_sum.273), channel_id=3, replica_groups=mesh['groups'=2,'context_0'=4,'context_1'=16,'context_2'=2] {'context_1'}, dimensions={0}, use_global_device_ids=true | all-gather | bytes 348160 | tf_op jit(solution)/shard_map/all_gather | solution.py:40
  195.3 13.1 %all-gather.2 = f32[10240]{0:T(1024)S(1)} all-gather(f32[5120]{0:T(1024)S(1)} %reduce_sum.274), channel_id=4, replica_groups=mesh['groups'=2,'context_0'=4,'context_1'=16,'context_2'=2] {'context_2'}, dimensions={0}, use_global_device_ids=true | all-gather | bytes 61440 | tf_op jit(solution)/shard_map/all_gather | solution.py:40
  209.1 1.6 slice_add_fusion.1
  215.4 9.1 %all-gather.3 = f32[4096]{0:T(1024)S(1)} all-gather(f32[1024]{0:T(1024)S(1)} %get-tuple-element.27), channel_id=5, replica_groups=mesh['groups'=2,'context_0'=4,'context_1'=16,'context_2'=2] {'context_0'}, dimensions={0}, use_global_device_ids=true | all-gather | bytes 20480 | tf_op jit(solution)/shard_map/all_gather | solution.py:40
  224.6 19.4 %all-gather.4 = f32[16384]{0:T(1024)S(1)} all-gather(f32[1024]{0:T(1024)S(1)} %reduce_sum.277), channel_id=6, replica_groups=mesh['groups'=2,'context_0'=4,'context_1'=16,'context_2'=2] {'context_1'}, dimensions={0}, use_global_device_ids=true | all-gather | bytes 69632 | tf_op jit(solution)/shard_map/all_gather | solution.py:40
  244.1 11.7 %all-gather.5 = f32[2048]{0:T(1024)S(1)} all-gather(f32[1024]{0:T(1024)S(1)} %reduce_sum.278), channel_id=7, replica_groups=mesh['groups'=2,'context_0'=4,'context_1'=16,'context_2'=2] {'context_2'}, dimensions={0}, use_global_device_ids=true | all-gather | bytes 12288 | tf_op jit(solution)/shard_map/all_gather | solution.py:40
  (268 shorter events, 30.7 us)
Async XLA Ops:
  0.6 5.7 %copy-start = (s32[16384]{0:T(1024)S(1)}, s32[16384]{0:T(1024)}, u32[]{:S(2)}) copy-start(s32[16384]{0:T(1024)} %param.14) | copy-start | bytes 196612
  0.6 2.0 copy-start.2
  0.7 5.5 %copy-start.82 = (s32[128]{0:T(128)}, s32[128]{0:T(128)S(1)}, u32[]{:S(2)}) copy-start(s32[128]{0:T(128)S(1)} %and_select_fusion.7) | copy-start | bytes 1540
  0.7 5.6 %copy-start.77 = (s32[128]{0:T(128)}, s32[128]{0:T(128)S(1)}, u32[]{:S(2)}) copy-start(s32[128]{0:T(128)S(1)} %and_select_fusion.10) | copy-start | bytes 1540
  2.7 5.4 %copy-start.59 = (bf16[128,1024]{1,0:T(8,128)(2,1)S(1)}, bf16[128,1024]{1,0:T(8,128)(2,1)}, u32[]{:S(2)}) copy-start(bf16[128,1024]{1,0:T(8,128)(2,1)} %param.9) | copy-start | bytes 786436
  2.7 6.5 %copy-start.72 = (f32[1024]{0:T(1024)S(1)}, f32[1024]{0:T(1024)}, u32[]{:S(2)}) copy-start(f32[1024]{0:T(1024)} %param.13) | copy-start | bytes 12292
  9.2 21.0 %copy-start.35 = (bf16[128,1024]{1,0:T(8,128)(2,1)S(1)}, bf16[128,1024]{1,0:T(8,128)(2,1)}, u32[]{:S(2)}) copy-start(bf16[128,1024]{1,0:T(8,128)(2,1)} %param.10) | copy-start | bytes 786436
  9.2 21.4 %copy-start.26 = (bf16[128,5120]{1,0:T(8,128)(2,1)S(1)}, bf16[128,5120]{1,0:T(8,128)(2,1)}, u32[]{:S(2)}) copy-start(bf16[128,5120]{1,0:T(8,128)(2,1)} %param.8) | copy-start | bytes 3932164
  9.7 32.3 %copy-start.14 = (bf16[128,1024]{1,0:T(8,128)(2,1)}, bf16[128,1024]{1,0:T(8,128)(2,1)S(1)}, u32[]{:S(2)}) copy-start(bf16[128,1024]{1,0:T(8,128)(2,1)S(1)} %copy.202) | copy-start | bytes 786436
  9.7 32.3 %collective-permute-start = (bf16[128,1024]{1,0:T(8,128)(2,1)S(1)}, bf16[128,1024]{1,0:T(8,128)(2,1)}, u32[]{:S(2)}, u32[]{:S(2)}) collective-permute-start(bf16[128,1024]{1,0:T(8,128)(2,1)S(1)} %copy.202), channel_id=1, source_target_pairs={{0,1},{1,0},{2,3},{3,2},{4,5},{5,4},{6,7},{7,6},{8,9},{9,8},{10,11... | collective-permute-start | bytes 786440 | tf_op jit(solution)/shard_map/ppermute | solution.py:27
  30.3 18.8 %collective-permute-start.2 = (bf16[128,1024]{1,0:T(8,128)(2,1)S(1)}, bf16[128,1024]{1,0:T(8,128)(2,1)}, u32[]{:S(2)}, u32[]{:S(2)}) collective-permute-start(bf16[128,1024]{1,0:T(8,128)(2,1)S(1)} %copy-done.35), channel_id=1, source_target_pairs={{0,1},{1,0},{2,3},{3,2},{4,5},{5,4},{6,7},{7,6},{8,9},{9,8},{10,11... | collective-permute-start | bytes 786440 | tf_op jit(solution)/shard_map/ppermute | solution.py:27
  32.1 2.2 copy-start.75
  35.7 3.2 %copy-start.78 = (s32[128]{0:T(128)S(1)}, s32[128]{0:T(128)}, u32[]{:S(2)}) copy-start(s32[128]{0:T(128)} %copy-done.77) | copy-start | bytes 1540
  35.7 3.2 %copy-start.83 = (s32[128]{0:T(128)S(1)}, s32[128]{0:T(128)}, u32[]{:S(2)}) copy-start(s32[128]{0:T(128)} %copy-done.82) | copy-start | bytes 1540
  35.7 3.3 %copy-start.79 = (s32[128]{0:T(128)S(1)}, s32[128]{0:T(128)}, u32[]{:S(2)}) copy-start(s32[128]{0:T(128)} %get-tuple-element.31) | copy-start | bytes 1540
  35.7 3.3 %copy-start.81 = (s32[128]{0:T(128)S(1)}, s32[128]{0:T(128)}, u32[]{:S(2)}) copy-start(s32[128]{0:T(128)} %copy-done.80) | copy-start | bytes 1540
  39.2 78.5 %copy-start.71 = (pred[128,512]{0,1:T(8,128)(4,1)}, pred[128,512]{0,1:T(8,128)(4,1)S(1)}, u32[]{:S(2)}) copy-start(pred[128,512]{0,1:T(8,128)(4,1)S(1)} %compare_and_fusion) | copy-start | bytes 196612
  43.8 15.2 %collective-permute-start.1 = (bf16[256,1024]{1,0:T(8,128)(2,1)}, bf16[256,1024]{1,0:T(8,128)(2,1)}, u32[]{:S(2)}, u32[]{:S(2)}) collective-permute-start(bf16[256,1024]{1,0:T(8,128)(2,1)} %pad_maximum_fusion.3), channel_id=1, source_target_pairs={{0,2},{2,0},{1,3},{3,1},{4,6},{6,4},{5,7},{7,5},{8,10},{10,8},{9,1... | collective-permute-start | bytes 1572872 | tf_op jit(solution)/shard_map/ppermute | solution.py:27
  48.0 4.4 %copy-start.41 = (bf16[128,640]{1,0:T(8,128)(2,1)S(1)}, bf16[128,640]{1,0:T(8,128)(2,1)}, u32[]{:S(2)}) copy-start(bf16[128,640]{1,0:T(8,128)(2,1)} %get-tuple-element.50) | copy-start | bytes 491524
  49.0 4.2 %copy-start.40 = (bf16[128,640]{1,0:T(8,128)(2,1)S(1)}, bf16[128,640]{1,0:T(8,128)(2,1)}, u32[]{:S(2)}) copy-start(bf16[128,640]{1,0:T(8,128)(2,1)} %get-tuple-element.49) | copy-start | bytes 491524
  49.0 5.0 %copy-start.39 = (bf16[128,640]{1,0:T(8,128)(2,1)S(1)}, bf16[128,640]{1,0:T(8,128)(2,1)}, u32[]{:S(2)}) copy-start(bf16[128,640]{1,0:T(8,128)(2,1)} %get-tuple-element.48) | copy-start | bytes 491524
  49.0 5.8 %copy-start.38 = (bf16[128,640]{1,0:T(8,128)(2,1)S(1)}, bf16[128,640]{1,0:T(8,128)(2,1)}, u32[]{:S(2)}) copy-start(bf16[128,640]{1,0:T(8,128)(2,1)} %get-tuple-element.47) | copy-start | bytes 491524
  49.0 6.6 %copy-start.37 = (bf16[128,640]{1,0:T(8,128)(2,1)S(1)}, bf16[128,640]{1,0:T(8,128)(2,1)}, u32[]{:S(2)}) copy-start(bf16[128,640]{1,0:T(8,128)(2,1)} %get-tuple-element.46) | copy-start | bytes 491524
  49.0 7.4 %copy-start.36 = (bf16[128,640]{1,0:T(8,128)(2,1)S(1)}, bf16[128,640]{1,0:T(8,128)(2,1)}, u32[]{:S(2)}) copy-start(bf16[128,640]{1,0:T(8,128)(2,1)} %get-tuple-element.45) | copy-start | bytes 491524
  50.9 8.0 %copy-start.15 = (bf16[128,1024]{1,0:T(8,128)(2,1)S(1)}, bf16[128,1024]{1,0:T(8,128)(2,1)}, u32[]{:S(2)}) copy-start(bf16[128,1024]{1,0:T(8,128)(2,1)} %copy-done.14) | copy-start | bytes 786436
  50.9 17.4 %collective-permute-start.3 = (bf16[256,1024]{1,0:T(8,128)(2,1)}, bf16[256,1024]{1,0:T(8,128)(2,1)}, u32[]{:S(2)}, u32[]{:S(2)}) collective-permute-start(bf16[256,1024]{1,0:T(8,128)(2,1)} %pad_maximum_fusion.4), channel_id=1, source_target_pairs={{0,2},{2,0},{1,3},{3,1},{4,6},{6,4},{5,7},{7,5},{8,10},{10,8},{9,1... | collective-permute-start | bytes 1572872 | tf_op jit(solution)/shard_map/ppermute | solution.py:27
  57.2 2.9 %copy-start.56 = (bf16[128,640]{0,1:T(8,128)(2,1)S(1)}, bf16[128,640]{0,1:T(8,128)(2,1)}, u32[]{:S(2)}) copy-start(bf16[128,640]{0,1:T(8,128)(2,1)} %get-tuple-element.44) | copy-start | bytes 491524
  60.2 22.2 %copy-start.12 = (bf16[512,1024]{1,0:T(8,128)(2,1)}, bf16[512,1024]{1,0:T(8,128)(2,1)S(1)}, u32[]{:S(2)}) copy-start(bf16[512,1024]{1,0:T(8,128)(2,1)S(1)} %pad_maximum_fusion.2) | copy-start | bytes 3145732
  60.2 10.1 %copy-start.70 = (bf16[128,640]{0,1:T(8,128)(2,1)S(1)}, bf16[128,640]{0,1:T(8,128)(2,1)}, u32[]{:S(2)}) copy-start(bf16[128,640]{0,1:T(8,128)(2,1)} %copy.318) | copy-start | bytes 491524
  70.3 1.8 copy-start.18
  74.4 2.6 copy-start.33
  74.4 3.3 %copy-start.53 = (bf16[128,640]{0,1:T(8,128)(2,1)S(1)}, bf16[128,640]{0,1:T(8,128)(2,1)}, u32[]{:S(2)}) copy-start(bf16[128,640]{0,1:T(8,128)(2,1)} %get-tuple-element.43) | copy-start | bytes 491524
  79.3 1.8 copy-start.20
  84.8 1.9 copy-start.21
  90.6 1.9 copy-start.22
  92.5 3.0 %copy-start.47 = (bf16[128,640]{0,1:T(8,128)(2,1)S(1)}, bf16[128,640]{0,1:T(8,128)(2,1)}, u32[]{:S(2)}) copy-start(bf16[128,640]{0,1:T(8,128)(2,1)} %get-tuple-element.40) | copy-start | bytes 491524
  98.1 1.9 copy-start.23
  100.0 3.0 %copy-start.45 = (bf16[128,640]{0,1:T(8,128)(2,1)S(1)}, bf16[128,640]{0,1:T(8,128)(2,1)}, u32[]{:S(2)}) copy-start(bf16[128,640]{0,1:T(8,128)(2,1)} %get-tuple-element.39) | copy-start | bytes 491524
  105.4 1.9 copy-start.24
  107.3 3.0 %copy-start.43 = (bf16[128,640]{0,1:T(8,128)(2,1)S(1)}, bf16[128,640]{0,1:T(8,128)(2,1)}, u32[]{:S(2)}) copy-start(bf16[128,640]{0,1:T(8,128)(2,1)} %get-tuple-element.38) | copy-start | bytes 491524
  112.8 1.9 copy-start.25
  114.7 3.0 %copy-start.42 = (bf16[128,640]{0,1:T(8,128)(2,1)S(1)}, bf16[128,640]{0,1:T(8,128)(2,1)}, u32[]{:S(2)}) copy-start(bf16[128,640]{0,1:T(8,128)(2,1)} %get-tuple-element.37) | copy-start | bytes 491524
  120.2 1.9 copy-start.19
  122.1 1.8 copy-start.13
  122.3 1.8 copy-start.30
  126.5 3.3 %copy-start.3 = (f32[128,40,2,64]{0,3,2,1:T(8,128)}, f32[128,40,2,64]{0,3,2,1:T(8,128)S(1)}, u32[]{:S(2)}) copy-start(f32[128,40,2,64]{0,3,2,1:T(8,128)S(1)} %pad_maximum_fusion) | copy-start | bytes 7864324
  126.5 3.3 %copy-start.16 = (f32[512,1024]{0,1:T(8,128)S(1)}, f32[512,1024]{0,1:T(8,128)}, u32[]{:S(2)}) copy-start(f32[512,1024]{0,1:T(8,128)} %fusion.73) | copy-start | bytes 6291460
  126.5 3.3 %copy-start.54 = (bf16[128,640]{0,1:T(8,128)(2,1)S(1)}, bf16[128,640]{0,1:T(8,128)(2,1)}, u32[]{:S(2)}) copy-start(bf16[128,640]{0,1:T(8,128)(2,1)} %get-tuple-element.43) | copy-start | bytes 491524
  126.5 3.7 %copy-start.51 = (bf16[128,640]{0,1:T(8,128)(2,1)S(1)}, bf16[128,640]{0,1:T(8,128)(2,1)}, u32[]{:S(2)}) copy-start(bf16[128,640]{0,1:T(8,128)(2,1)} %get-tuple-element.42) | copy-start | bytes 491524
  132.8 2.9 %copy-start.55 = (bf16[128,640]{0,1:T(8,128)(2,1)S(1)}, bf16[128,640]{0,1:T(8,128)(2,1)}, u32[]{:S(2)}) copy-start(bf16[128,640]{0,1:T(8,128)(2,1)} %get-tuple-element.43) | copy-start | bytes 491524
  132.8 2.9 %copy-start.64 = (bf16[128,640]{0,1:T(8,128)(2,1)S(1)}, bf16[128,640]{0,1:T(8,128)(2,1)}, u32[]{:S(2)}) copy-start(bf16[128,640]{0,1:T(8,128)(2,1)} %copy.319) | copy-start | bytes 491524
  135.5 2.7 %copy-start.52 = (bf16[128,640]{0,1:T(8,128)(2,1)S(1)}, bf16[128,640]{0,1:T(8,128)(2,1)}, u32[]{:S(2)}) copy-start(bf16[128,640]{0,1:T(8,128)(2,1)} %get-tuple-element.42) | copy-start | bytes 491524
  135.5 2.7 %copy-start.69 = (bf16[128,640]{0,1:T(8,128)(2,1)S(1)}, bf16[128,640]{0,1:T(8,128)(2,1)}, u32[]{:S(2)}) copy-start(bf16[128,640]{0,1:T(8,128)(2,1)} %copy.320) | copy-start | bytes 491524
  135.5 73.6 %collective-permute-start.4 = (bf16[256,1024]{0,1:T(8,128)(2,1)}, bf16[256,1024]{0,1:T(8,128)(2,1)}, u32[]{:S(2)}, u32[]{:S(2)}) collective-permute-start(bf16[256,1024]{0,1:T(8,128)(2,1)} %slice.375), channel_id=1, source_target_pairs={{0,2},{2,0},{1,3},{3,1},{4,6},{6,4},{5,7},{7,5},{8,10},{10,8},{9,1... | collective-permute-start | bytes 1572872 | tf_op jit(solution)/shard_map/ppermute | solution.py:27
  138.2 2.5 copy-start.68
  140.7 2.5 copy-start.67
  143.1 2.4 copy-start.66
  145.6 2.5 copy-start.65
  148.0 2.4 copy-start.62
  155.0 56.2 %collective-permute-start.6 = (bf16[256,1024]{0,1:T(8,128)(2,1)}, bf16[256,1024]{0,1:T(8,128)(2,1)S(1)}, u32[]{:S(2)}, u32[]{:S(2)}) collective-permute-start(bf16[256,1024]{0,1:T(8,128)(2,1)} %slice.374), channel_id=1, source_target_pairs={{0,2},{2,0},{1,3},{3,1},{4,6},{6,4},{5,7},{7,5},{8,10},{10,8},{9,1... | collective-permute-start | bytes 1572872 | tf_op jit(solution)/shard_map/ppermute | solution.py:27
  209.1 2.1 copy-start.34
  210.7 1.7 collective-permute-start.5
  211.4 3.1 %collective-permute-start.7 = (bf16[128,1024]{0,1:T(8,128)(2,1)S(1)}, bf16[128,1024]{0,1:T(8,128)(2,1)S(1)}, u32[]{:S(2)}, u32[]{:S(2)}) collective-permute-start(bf16[128,1024]{0,1:T(8,128)(2,1)S(1)} %slice.376), channel_id=1, source_target_pairs={{0,1},{1,0},{2,3},{3,2},{4,5},{5,4},{6,7},{7,6},{8,9},{9,8},{10,11... | collective-permute-start | bytes 786440 | tf_op jit(solution)/shard_map/ppermute | solution.py:27
  213.5 42.9 %copy-start.1 = (s32[16384]{0:T(1024)S(1)}, s32[16384]{0:T(1024)}, u32[]{:S(2)}) copy-start(s32[16384]{0:T(1024)} %param.14) | copy-start | bytes 196612
  (28 other events, 31.8 us)
